TPU v7x, 32 devices: a whole 2x2x4 slice. The times are simulated.
32 devices in a mesh: mp: 2 (over core), dev: 16 (over z, y, x).
Axes of the slice: x: 2, y: 2, z: 4, core: 2. Of those that a mesh axis runs over, the one named last changes fastest.
Arguments:
- spectrum: float32 [1024, 8192], P(None, ('mp', 'dev')), may hold values from 0.05 to 1
- water_mask: int32 [8192], P(('mp', 'dev')), may hold values 0 or 1
- courant: float32 [2, 1024], replicated, may hold values from 0.05 to 0.3
- stencil_sign: int32 [2, 1024], replicated, may hold values from 0 to 1
- quad_index: int32 [4, 1024, 2], replicated, may hold values from 0 to 1023
- quad_weight: float32 [4, 1024, 2], replicated, may hold values from 0.2 to 1
- nonlinear: float32 [1024], replicated, may hold values from 0.01 to 0.1
- stokes_table: bfloat16 [128, 1024], replicated, may hold values from -0.1875 to 0.1875
- point_index: int32 [4, 8192], P(None, ('mp', 'dev')), may hold values from 0 to 4095, as said below
- point_weight: float32 [4, 8192], P(None, ('mp', 'dev')), may hold values from 0.1 to 0.4
- ocean_index: int32 [4, 4096], P(None, ('mp', 'dev')), may hold values from 0 to 8191, as said below
- ocean_weight: float32 [4, 4096], P(None, ('mp', 'dev')), may hold values from 0.1 to 0.4
- currents: float32 [2, 64, 4096], P(None, None, ('mp', 'dev')), may hold values from -3 to 3
- coriolis: float32 [4096], P(('mp', 'dev')), may hold values from 0.2 to 0.6
- mixing: float32 [64], replicated, may hold values from 0.05 to 0.2
- surface_weights: float32 [64], replicated, may hold values from 0.005 to 0.05
Outputs:
- spectrum_out: float32 [1024, 8192], P(None, ('mp', 'dev'))
- currents_out: float32 [2, 64, 4096], P(None, None, ('mp', 'dev'))
Inputs may be any that keep to these rules, and one draw needn't show every extreme that they name: `point_index`: entry j of point p names an ocean cell in row p // 256 plus -1, 0 or 1 and column (p % 256) // 2 plus -1, 0 or 1, both wrapping. `ocean_index`: entry j of cell c names a wave point in row c // 128 plus -1, 0 or 1 and column 2 (c % 128) plus -2 to 3, both wrapping.
All inputs are finite; a program needn't handle non-finite values. No bound on the sum of `water_mask` on one device may be relied on, other than what follows from the above.
Results may differ from a plain program's by a relative error of at most 0.0003.
The roundings to bfloat16 on the way count: a program that leaves them out, or rounds other values in their place, can miss the bound.
Values sent between devices are 32-bit elements; how exact they have to be, the bound alone decides.
A program may use at most 64 MiB of HBM per device.

v0:
```python
import jax
import jax.numpy as jnp
from jax import lax
from jax.sharding import PartitionSpec as P

K = 1024
L = 64
MX = 256
ROWS_DEV = 1
STEPS = 2
OX = 128


ocean_step_size = 0.5


def padded_2(cells, sides, width):
    for axis, dim in sides:
        count = lax.axis_size(axis)
        head = lax.slice_in_dim(cells, 0, width, axis=dim)
        tail = lax.slice_in_dim(cells, cells.shape[dim] - width, cells.shape[dim], axis=dim)
        cells = jnp.concatenate(
            [
                lax.ppermute(tail, axis, [(i, (i + 1) % count) for i in range(count)]),
                cells,
                lax.ppermute(head, axis, [((i + 1) % count, i) for i in range(count)]),
            ],
            axis=dim,
        )
    return cells


def advect(spectra, padded, point_flow, courant, stencil_sign):
    eastward = stencil_sign[0][:, None, None] == 1
    northward = stencil_sign[1][:, None, None] == 1
    sense_x = (2 * stencil_sign[0] - 1).astype(jnp.float32)[:, None, None]
    sense_y = (2 * stencil_sign[1] - 1).astype(jnp.float32)[:, None, None]
    behind_x = jnp.where(eastward, jnp.roll(spectra, 1, axis=2), jnp.roll(spectra, -1, axis=2))
    behind_y = jnp.where(northward, padded[:, :-2], padded[:, 2:])
    speed_x = courant[0][:, None, None] * (1.0 + 0.5 * jnp.tanh(sense_x * point_flow[0][None]))
    speed_y = courant[1][:, None, None] * (1.0 + 0.5 * jnp.tanh(sense_y * point_flow[1][None]))
    return spectra - speed_x * (spectra - behind_x) - speed_y * (spectra - behind_y)


def quad_table(row_index, weight, span_width):
    columns = jnp.arange(span_width, dtype=jnp.int32)[None, :]
    first_part = jnp.where(row_index[:, 0:1] == columns, weight[:, 0:1], 0.0)
    second = jnp.where(row_index[:, 1:2] == columns, weight[:, 1:2], 0.0)
    return (first_part + second).astype(jnp.bfloat16)


def spread_table(local_index, weight, wide_count):
    slots = jnp.arange(wide_count, dtype=jnp.int32)[:, None]
    total = jnp.zeros((wide_count, local_index.shape[1]), jnp.float32)
    for config in range(4):
        total = total + jnp.where(
            local_index[config][None, :] == slots, weight[config][None, :], 0.0
        )
    return total


def nonlinear_update(advected, interps, gain_rows, wet_row):
    total_sum = interps[0] + interps[1] + interps[2] + interps[3]
    pair_sum = interps[0] * interps[1] + interps[2] * interps[3]
    source = advected * advected * total_sum - advected * pair_sum
    return wet_row[None, :] * (advected + gain_rows[:, None] * source)


def vertical_mix(profile, mixing):
    above_level = jnp.concatenate([profile[:1], profile[:-1]], axis=0)
    below_level = jnp.concatenate([profile[1:], profile[-1:]], axis=0)
    return mixing[:, None, None] * (above_level - 2.0 * profile + below_level)


def ocean_prepare(zonal_flow, meridional, mixing):
    padded_zonal = padded_2(zonal_flow, ((("mp", "dev"), 1),), 1)
    vorticity = 0.5 * (jnp.roll(meridional, -1, axis=2) - jnp.roll(meridional, 1, axis=2)) - 0.5 * (
        padded_zonal[:, 2:] - padded_zonal[:, :-2]
    )
    return (vorticity, vertical_mix(zonal_flow, mixing), vertical_mix(meridional, mixing))


def ocean_advance(zonal_flow, meridional, tendency, stokes_drift, rotation):
    vorticity, mix_zonal, mix_meridional = tendency
    drift_x = stokes_drift[0]
    drift_y = stokes_drift[1]
    new_zonal = zonal_flow + ocean_step_size * (
        rotation[None] * (meridional + drift_y) + vorticity * drift_y + mix_zonal
    )
    new_meridional = meridional + ocean_step_size * (
        -rotation[None] * (zonal_flow + drift_x) - vorticity * drift_x + mix_meridional
    )
    return jnp.stack([new_zonal, new_meridional])


def transport(spectra, point_flow, courant, stencil_sign):
    comp_total = spectra.shape[0]
    map_grid = spectra.reshape(comp_total, -1, MX)
    padded = padded_2(map_grid, ((("mp", "dev"), 1),), 1)
    shifted = advect(map_grid, padded, point_flow.reshape(2, -1, MX), courant, stencil_sign)
    return shifted.reshape(comp_total, -1)


def sources(advected, quad_tables, nonlinear, wet_points):
    rounded = advected.astype(jnp.bfloat16)
    interps = [
        jnp.dot(quad_tables[config], rounded, preferred_element_type=jnp.float32)
        for config in range(4)
    ]
    return nonlinear_update(advected, interps, nonlinear, wet_points)


def local(
    spectrum,
    water_mask,
    courant,
    stencil_sign,
    quad_index,
    quad_weight,
    nonlinear,
    stokes_table,
    point_index,
    point_weight,
    ocean_index,
    ocean_weight,
    currents,
    coriolis,
    mixing,
    surface_weights,
):
    devices = lax.axis_size("mp") * lax.axis_size("dev")
    position = lax.axis_index(("mp", "dev"))
    local_points = spectrum.shape[1]
    local_cells = currents.shape[2]
    cell_local = jnp.mod(point_index - position * local_cells + OX, local_cells * devices)
    point_local = jnp.mod(ocean_index - position * local_points + MX, local_points * devices)
    surface_spread = spread_table(cell_local, point_weight, local_cells + 2 * OX)
    stokes_spread = spread_table(point_local, ocean_weight, local_points + 2 * MX)
    quad_tables = [quad_table(quad_index[config], quad_weight[config], K) for config in range(4)]
    wet_points = water_mask.astype(jnp.float32)
    rotation = coriolis.reshape(ROWS_DEV, OX)
    ocean_state = currents
    spectra = spectrum
    for step_index in range(STEPS):
        zonal_flow = ocean_state[0].reshape(L, ROWS_DEV, OX)
        meridional = ocean_state[1].reshape(L, ROWS_DEV, OX)
        surface = jnp.sum(surface_weights[None, :, None] * ocean_state, axis=1)
        surface_wide = padded_2(surface, ((("mp", "dev"), 1),), OX)
        point_flow = jnp.dot(surface_wide, surface_spread, precision=lax.Precision.HIGHEST)
        advected = transport(spectra, point_flow, courant, stencil_sign)
        spectra = sources(advected, quad_tables, nonlinear, wet_points)
        stokes = jnp.dot(
            stokes_table, spectra.astype(jnp.bfloat16), preferred_element_type=jnp.float32
        )
        stokes_wide = padded_2(stokes, ((("mp", "dev"), 1),), MX)
        stokes_drift = jnp.dot(stokes_wide, stokes_spread, precision=lax.Precision.HIGHEST)
        stokes_drift = stokes_drift.reshape(2, L, ROWS_DEV, OX)
        tendency = ocean_prepare(zonal_flow, meridional, mixing)
        ocean_state = ocean_advance(
            zonal_flow, meridional, tendency, stokes_drift, rotation
        ).reshape(2, L, ROWS_DEV * OX)
    return (spectra, ocean_state)


def solution(mesh):
    return jax.shard_map(
        local,
        mesh=mesh,
        in_specs=(
            P(None, ("mp", "dev")),
            P(("mp", "dev")),
            P(),
            P(),
            P(),
            P(),
            P(),
            P(),
            P(None, ("mp", "dev")),
            P(None, ("mp", "dev")),
            P(None, ("mp", "dev")),
            P(None, ("mp", "dev")),
            P(None, None, ("mp", "dev")),
            P(("mp", "dev")),
            P(),
            P(),
        ),
        out_specs=(P(None, ("mp", "dev")), P(None, None, ("mp", "dev"))),
        check_vma=False,
    )
```

profile of v0, /device:TPU:0, one launch (start us, length us, event | category | flops | bytes accessed | tf_op | source)
XLA Modules:
  0.0 145.0 jit_solution(2811001653742906922)
XLA Ops:
  0.6 1.6 %multiply_reduce_fusion = f32[2,128]{1,0:T(2,128)} fusion(f32[2,64,128]{2,1,0:T(8,128)} %param.28, f32[64]{0:T(128)} %param.31), kind=kLoop, calls=%fused_computation.108 | loop fusion | flops 32512 | bytes 66816 | tf_op jit(solution)/shard_map/reduce_sum | solution.py:147
  2.2 3.0 %collective-permute-start = (f32[2,128]{1,0:T(2,128)}, f32[2,128]{1,0:T(2,128)}, u32[]{:S(2)}, u32[]{:S(2)}) collective-permute-start(f32[2,128]{1,0:T(2,128)} %multiply_reduce_fusion), channel_id=1, source_target_pairs={{0,1},{1,2},{2,3},{3,4},{4,5},{5,6},{6,7},{7,8},{8,9},{9,10},{10,1... | collective-permute-start | bytes 3080 | tf_op jit(solution)/shard_map/ppermute | solution.py:24
  5.2 3.5 %collective-permute-start.1 = (f32[2,128]{1,0:T(2,128)}, f32[2,128]{1,0:T(2,128)}, u32[]{:S(2)}, u32[]{:S(2)}) collective-permute-start(f32[2,128]{1,0:T(2,128)} %multiply_reduce_fusion), channel_id=1, source_target_pairs={{1,0},{2,1},{3,2},{4,3},{5,4},{6,5},{7,6},{8,7},{9,8},{10,9},{11,1... | collective-permute-start | bytes 3080 | tf_op jit(solution)/shard_map/ppermute | solution.py:26
  10.4 5.3 %collective-permute-start.3 = (f32[1024,1,256]{0,2,1:T(8,128)S(1)}, f32[1024,1,256]{0,2,1:T(8,128)S(1)}, u32[]{:S(2)}, u32[]{:S(2)}) collective-permute-start(f32[1024,1,256]{0,2,1:T(8,128)S(1)} %bitcast.195), channel_id=1, source_target_pairs={{1,0},{2,1},{3,2},{4,3},{5,4},{6,5},{7,6},{8,7},{9,8},{10,9},{11,1... | collective-permute-start | bytes 3145736 | tf_op jit(solution)/shard_map/ppermute | solution.py:26
  28.2 2.1 %collective-permute-start.7 = (f32[64,1,128]{2,0,1:T(8,128)}, f32[64,1,128]{2,0,1:T(8,128)S(1)}, u32[]{:S(2)}, u32[]{:S(2)}) collective-permute-start(f32[64,1,128]{2,0,1:T(8,128)} %get-tuple-element.23), channel_id=1, source_target_pairs={{0,1},{1,2},{2,3},{3,4},{4,5},{5,6},{6,7},{7,8},{8,9},{9,10},{10,1... | collective-permute-start | bytes 98312 | tf_op jit(solution)/shard_map/ppermute | solution.py:24
  31.5 25.6 %collective-permute-done.2 = f32[1024,1,256]{0,2,1:T(8,128)S(1)} collective-permute-done((f32[1024,1,256]{0,2,1:T(8,128)S(1)}, f32[1024,1,256]{0,2,1:T(8,128)S(1)}, u32[]{:S(2)}, u32[]{:S(2)}) %collective-permute-start.2) | collective-permute-done | bytes 1048608 | tf_op jit(solution)/shard_map/ppermute | solution.py:24
  58.0 2.3 %fusion.1 = f32[1024,256]{0,1:T(8,128)S(1)} fusion(bf16[1024,256]{0,1:T(8,128)(2,1)S(1)} %get-tuple-element.12, f32[1024]{0:T(1024)S(1)} %bitcast.234, s32[1024]{0:T(1024)S(1)} %bitcast.226, f32[1024]{0:T(1024)S(1)} %bitcast.232, s32[1024]{0:T(1024)S(1)} %bitcast.224), kind=kOutput, calls=%fused_computation.13 | convolution fusion | flops 543162368 | bytes 1589248 | tf_op jit(solution)/shard_map/dot_general | solution.py:107
  60.3 2.3 %fusion.3 = f32[1024,256]{0,1:T(8,128)S(1)} fusion(bf16[1024,256]{0,1:T(8,128)(2,1)S(1)} %get-tuple-element.12, f32[1024]{0:T(1024)S(1)} %bitcast.244, s32[1024]{0:T(1024)S(1)} %bitcast.240, f32[1024]{0:T(1024)S(1)} %bitcast.246, s32[1024]{0:T(1024)S(1)} %bitcast.242), kind=kOutput, calls=%fused_computation.15 | convolution fusion | flops 543162368 | bytes 1589248 | tf_op jit(solution)/shard_map/dot_general | solution.py:107
  62.7 2.3 %fusion.7 = f32[1024,256]{0,1:T(8,128)S(1)} fusion(bf16[1024,256]{0,1:T(8,128)(2,1)S(1)} %get-tuple-element.12, f32[1024]{0:T(1024)S(1)} %bitcast.220, s32[1024]{0:T(1024)S(1)} %bitcast.216, f32[1024]{0:T(1024)S(1)} %bitcast.222, s32[1024]{0:T(1024)S(1)} %bitcast.218), kind=kOutput, calls=%fused_computation.19 | convolution fusion | flops 543162368 | bytes 1589248 | tf_op jit(solution)/shard_map/dot_general | solution.py:107
  65.0 1.9 %add_multiply_fusion.1 = f32[1024,256]{0,1:T(8,128)S(1)} fusion(f32[1024,256]{0,1:T(8,128)S(1)} %get-tuple-element.13, f32[1024,256]{0,1:T(8,128)S(1)} %fusion.7, f32[1024,256]{0,1:T(8,128)S(1)} %fusion.1, f32[1024,256]{0,1:T(8,128)S(1)} %fusion.3, f32[1024]{0:T(1024)S(1)} %copy-done.39, f32[256]{0:T(256)S(1)} %convert_element_type.49, ...), kind=kOutput, calls=%fused_computation.41 | convolution fusion | flops 546570240 | bytes 5788672 | tf_op jit(solution)/shard_map/dot_general | solution.py:107
  67.2 2.5 %collective-permute-start.4 = (f32[128,256]{0,1:T(8,128)S(1)}, f32[128,256]{0,1:T(8,128)S(1)}, u32[]{:S(2)}, u32[]{:S(2)}) collective-permute-start(f32[128,256]{0,1:T(8,128)S(1)} %convolution_bitcast_fusion.1), channel_id=1, source_target_pairs={{0,1},{1,2},{2,3},{3,4},{4,5},{5,6},{6,7},{7,8},{8,9},{9,10},{10,1... | collective-permute-start | bytes 393224 | tf_op jit(solution)/shard_map/ppermute | solution.py:24
  69.8 2.9 %collective-permute-start.5 = (f32[128,256]{0,1:T(8,128)S(1)}, f32[128,256]{0,1:T(8,128)S(1)}, u32[]{:S(2)}, u32[]{:S(2)}) collective-permute-start(f32[128,256]{0,1:T(8,128)S(1)} %convolution_bitcast_fusion.1), channel_id=1, source_target_pairs={{1,0},{2,1},{3,2},{4,3},{5,4},{6,5},{7,6},{8,7},{9,8},{10,9},{11,1... | collective-permute-start | bytes 393224 | tf_op jit(solution)/shard_map/ppermute | solution.py:26
  73.0 24.4 %collective-permute-done.4 = f32[128,256]{0,1:T(8,128)S(1)} collective-permute-done((f32[128,256]{0,1:T(8,128)S(1)}, f32[128,256]{0,1:T(8,128)S(1)}, u32[]{:S(2)}, u32[]{:S(2)}) %collective-permute-start.4) | collective-permute-done | bytes 131104 | tf_op jit(solution)/shard_map/ppermute | solution.py:24
  99.6 2.6 %collective-permute-start.8 = (f32[2,128]{1,0:T(2,128)S(1)}, f32[2,128]{1,0:T(2,128)S(1)}, u32[]{:S(2)}, u32[]{:S(2)}) collective-permute-start(f32[2,128]{1,0:T(2,128)S(1)} %fusion.73), channel_id=1, source_target_pairs={{0,1},{1,2},{2,3},{3,4},{4,5},{5,6},{6,7},{7,8},{8,9},{9,10},{10,1... | collective-permute-start | bytes 3080 | tf_op jit(solution)/shard_map/ppermute | solution.py:24
  102.2 2.8 %collective-permute-start.9 = (f32[2,128]{1,0:T(2,128)S(1)}, f32[2,128]{1,0:T(2,128)S(1)}, u32[]{:S(2)}, u32[]{:S(2)}) collective-permute-start(f32[2,128]{1,0:T(2,128)S(1)} %fusion.73), channel_id=1, source_target_pairs={{1,0},{2,1},{3,2},{4,3},{5,4},{6,5},{7,6},{8,7},{9,8},{10,9},{11,1... | collective-permute-start | bytes 3080 | tf_op jit(solution)/shard_map/ppermute | solution.py:26
  105.2 15.5 %collective-permute-done.8 = f32[2,128]{1,0:T(2,128)S(1)} collective-permute-done((f32[2,128]{1,0:T(2,128)S(1)}, f32[2,128]{1,0:T(2,128)S(1)}, u32[]{:S(2)}, u32[]{:S(2)}) %collective-permute-start.8) | collective-permute-done | bytes 1056 | tf_op jit(solution)/shard_map/ppermute | solution.py:24
  120.6 2.5 %collective-permute-start.15 = (f32[64,1,128]{2,0,1:T(8,128)S(1)}, f32[64,1,128]{2,0,1:T(8,128)S(1)}, u32[]{:S(2)}, u32[]{:S(2)}) collective-permute-start(f32[64,1,128]{2,0,1:T(8,128)S(1)} %get-tuple-element.10), channel_id=1, source_target_pairs={{0,1},{1,2},{2,3},{3,4},{4,5},{5,6},{6,7},{7,8},{8,9},{9,10},{10,1... | collective-permute-start | bytes 98312 | tf_op jit(solution)/shard_map/ppermute | solution.py:24
  125.1 2.3 %fusion = f32[1024,256]{0,1:T(8,128)S(1)} fusion(bf16[1024,256]{0,1:T(8,128)(2,1)S(1)} %get-tuple-element.8, f32[1024]{0:T(1024)S(1)} %bitcast.235, s32[1024]{0:T(1024)S(1)} %bitcast.227, f32[1024]{0:T(1024)S(1)} %bitcast.233, s32[1024]{0:T(1024)S(1)} %bitcast.225), kind=kOutput, calls=%fused_computation.12 | convolution fusion | flops 543162368 | bytes 1589248 | tf_op jit(solution)/shard_map/dot_general | solution.py:107
  127.4 2.3 %fusion.2 = f32[1024,256]{0,1:T(8,128)S(1)} fusion(bf16[1024,256]{0,1:T(8,128)(2,1)S(1)} %get-tuple-element.8, f32[1024]{0:T(1024)S(1)} %bitcast.245, s32[1024]{0:T(1024)S(1)} %bitcast.241, f32[1024]{0:T(1024)S(1)} %bitcast.247, s32[1024]{0:T(1024)S(1)} %bitcast.243), kind=kOutput, calls=%fused_computation.14 | convolution fusion | flops 543162368 | bytes 1589248 | tf_op jit(solution)/shard_map/dot_general | solution.py:107
  129.7 2.3 %fusion.6 = f32[1024,256]{0,1:T(8,128)S(1)} fusion(bf16[1024,256]{0,1:T(8,128)(2,1)S(1)} %get-tuple-element.8, f32[1024]{0:T(1024)S(1)} %bitcast.221, s32[1024]{0:T(1024)S(1)} %bitcast.217, f32[1024]{0:T(1024)S(1)} %bitcast.223, s32[1024]{0:T(1024)S(1)} %bitcast.219), kind=kOutput, calls=%fused_computation.18 | convolution fusion | flops 543162368 | bytes 1589248 | tf_op jit(solution)/shard_map/dot_general | solution.py:107
  132.0 1.8 %add_multiply_fusion = f32[1024,256]{0,1:T(8,128)S(1)} fusion(f32[1024,256]{0,1:T(8,128)S(1)} %get-tuple-element.9, f32[1024,256]{0,1:T(8,128)S(1)} %fusion.6, f32[1024,256]{0,1:T(8,128)S(1)} %fusion, f32[1024,256]{0,1:T(8,128)S(1)} %fusion.2, f32[1024]{0:T(1024)S(1)} %copy-done.39, f32[256]{0:T(256)S(1)} %convert_element_type.49, ...), kind=kOutput, calls=%fused_computation.40 | convolution fusion | flops 546570240 | bytes 5788672 | tf_op jit(solution)/shard_map/dot_general | solution.py:107
  134.2 2.9 %collective-permute-start.12 = (f32[128,256]{0,1:T(8,128)S(1)}, f32[128,256]{0,1:T(8,128)S(1)}, u32[]{:S(2)}, u32[]{:S(2)}) collective-permute-start(f32[128,256]{0,1:T(8,128)S(1)} %convolution_bitcast_fusion), channel_id=1, source_target_pairs={{0,1},{1,2},{2,3},{3,4},{4,5},{5,6},{6,7},{7,8},{8,9},{9,10},{10,1... | collective-permute-start | bytes 393224 | tf_op jit(solution)/shard_map/ppermute | solution.py:24
  137.1 2.5 %collective-permute-start.13 = (f32[128,256]{0,1:T(8,128)S(1)}, f32[128,256]{0,1:T(8,128)S(1)}, u32[]{:S(2)}, u32[]{:S(2)}) collective-permute-start(f32[128,256]{0,1:T(8,128)S(1)} %convolution_bitcast_fusion), channel_id=1, source_target_pairs={{1,0},{2,1},{3,2},{4,3},{5,4},{6,5},{7,6},{8,7},{9,8},{10,9},{11,1... | collective-permute-start | bytes 393224 | tf_op jit(solution)/shard_map/ppermute | solution.py:26
  140.9 2.2 %collective-permute-done.12 = f32[128,256]{0,1:T(8,128)S(1)} collective-permute-done((f32[128,256]{0,1:T(8,128)S(1)}, f32[128,256]{0,1:T(8,128)S(1)}, u32[]{:S(2)}, u32[]{:S(2)}) %collective-permute-start.12) | collective-permute-done | bytes 131104 | tf_op jit(solution)/shard_map/ppermute | solution.py:24
  (147 shorter events, 24.2 us)
Async XLA Ops:
  0.6 66.3 %copy-start = (bf16[128,1024]{1,0:T(8,128)(2,1)S(1)}, bf16[128,1024]{1,0:T(8,128)(2,1)}, u32[]{:S(2)}) copy-start(bf16[128,1024]{1,0:T(8,128)(2,1)} %param.23) | copy-start | bytes 786436
  2.2 26.0 %collective-permute-start = (f32[2,128]{1,0:T(2,128)}, f32[2,128]{1,0:T(2,128)}, u32[]{:S(2)}, u32[]{:S(2)}) collective-permute-start(f32[2,128]{1,0:T(2,128)} %multiply_reduce_fusion), channel_id=1, source_target_pairs={{0,1},{1,2},{2,3},{3,4},{4,5},{5,6},{6,7},{7,8},{8,9},{9,10},{10,1... | collective-permute-start | bytes 3080 | tf_op jit(solution)/shard_map/ppermute | solution.py:24
  5.2 25.1 %collective-permute-start.1 = (f32[2,128]{1,0:T(2,128)}, f32[2,128]{1,0:T(2,128)}, u32[]{:S(2)}, u32[]{:S(2)}) collective-permute-start(f32[2,128]{1,0:T(2,128)} %multiply_reduce_fusion), channel_id=1, source_target_pairs={{1,0},{2,1},{3,2},{4,3},{5,4},{6,5},{7,6},{8,7},{9,8},{10,9},{11,1... | collective-permute-start | bytes 3080 | tf_op jit(solution)/shard_map/ppermute | solution.py:26
  10.3 46.8 %collective-permute-start.2 = (f32[1024,1,256]{0,2,1:T(8,128)S(1)}, f32[1024,1,256]{0,2,1:T(8,128)S(1)}, u32[]{:S(2)}, u32[]{:S(2)}) collective-permute-start(f32[1024,1,256]{0,2,1:T(8,128)S(1)} %bitcast.194), channel_id=1, source_target_pairs={{0,1},{1,2},{2,3},{3,4},{4,5},{5,6},{6,7},{7,8},{8,9},{9,10},{10,1... | collective-permute-start | bytes 3145736 | tf_op jit(solution)/shard_map/ppermute | solution.py:24
  10.4 46.7 %collective-permute-start.3 = (f32[1024,1,256]{0,2,1:T(8,128)S(1)}, f32[1024,1,256]{0,2,1:T(8,128)S(1)}, u32[]{:S(2)}, u32[]{:S(2)}) collective-permute-start(f32[1024,1,256]{0,2,1:T(8,128)S(1)} %bitcast.195), channel_id=1, source_target_pairs={{1,0},{2,1},{3,2},{4,3},{5,4},{6,5},{7,6},{8,7},{9,8},{10,9},{11,1... | collective-permute-start | bytes 3145736 | tf_op jit(solution)/shard_map/ppermute | solution.py:26
  16.3 82.1 %collective-permute-start.6 = (f32[64,1,128]{2,0,1:T(8,128)}, f32[64,1,128]{2,0,1:T(8,128)}, u32[]{:S(2)}, u32[]{:S(2)}) collective-permute-start(f32[64,1,128]{2,0,1:T(8,128)} %get-tuple-element.23), channel_id=1, source_target_pairs={{1,0},{2,1},{3,2},{4,3},{5,4},{6,5},{7,6},{8,7},{9,8},{10,9},{11,1... | collective-permute-start | bytes 98312 | tf_op jit(solution)/shard_map/ppermute | solution.py:26
  24.2 73.2 %copy-start.31 = (s32[128]{0:T(128)}, s32[128]{0:T(128)S(1)}, u32[]{:S(2)}) copy-start(s32[128]{0:T(128)S(1)} %get-tuple-element.86) | copy-start | bytes 1540
  24.2 73.2 %copy-start.33 = (s32[128]{0:T(128)}, s32[128]{0:T(128)S(1)}, u32[]{:S(2)}) copy-start(s32[128]{0:T(128)S(1)} %get-tuple-element.87) | copy-start | bytes 1540
  24.3 73.2 %copy-start.35 = (s32[128]{0:T(128)}, s32[128]{0:T(128)S(1)}, u32[]{:S(2)}) copy-start(s32[128]{0:T(128)S(1)} %get-tuple-element.88) | copy-start | bytes 1540
  24.3 73.2 %copy-start.37 = (s32[128]{0:T(128)}, s32[128]{0:T(128)S(1)}, u32[]{:S(2)}) copy-start(s32[128]{0:T(128)S(1)} %get-tuple-element.89) | copy-start | bytes 1540
  27.8 29.3 %copy-start.10 = (f32[1024,1]{0,1:T(1,128)S(1)}, f32[1024,1]{0,1:T(1,128)}, u32[]{:S(2)}) copy-start(f32[1024,1]{0,1:T(1,128)} %get-tuple-element.18) | copy-start | bytes 12292
  27.8 29.3 %copy-start.11 = (f32[1024,1]{0,1:T(1,128)S(1)}, f32[1024,1]{0,1:T(1,128)}, u32[]{:S(2)}) copy-start(f32[1024,1]{0,1:T(1,128)} %get-tuple-element.19) | copy-start | bytes 12292
  28.2 70.2 %collective-permute-start.7 = (f32[64,1,128]{2,0,1:T(8,128)}, f32[64,1,128]{2,0,1:T(8,128)S(1)}, u32[]{:S(2)}, u32[]{:S(2)}) collective-permute-start(f32[64,1,128]{2,0,1:T(8,128)} %get-tuple-element.23), channel_id=1, source_target_pairs={{0,1},{1,2},{2,3},{3,4},{4,5},{5,6},{6,7},{7,8},{8,9},{9,10},{10,1... | collective-permute-start | bytes 98312 | tf_op jit(solution)/shard_map/ppermute | solution.py:24
  67.2 30.2 %collective-permute-start.4 = (f32[128,256]{0,1:T(8,128)S(1)}, f32[128,256]{0,1:T(8,128)S(1)}, u32[]{:S(2)}, u32[]{:S(2)}) collective-permute-start(f32[128,256]{0,1:T(8,128)S(1)} %convolution_bitcast_fusion.1), channel_id=1, source_target_pairs={{0,1},{1,2},{2,3},{3,4},{4,5},{5,6},{6,7},{7,8},{8,9},{9,10},{10,1... | collective-permute-start | bytes 393224 | tf_op jit(solution)/shard_map/ppermute | solution.py:24
  69.8 27.7 %collective-permute-start.5 = (f32[128,256]{0,1:T(8,128)S(1)}, f32[128,256]{0,1:T(8,128)S(1)}, u32[]{:S(2)}, u32[]{:S(2)}) collective-permute-start(f32[128,256]{0,1:T(8,128)S(1)} %convolution_bitcast_fusion.1), channel_id=1, source_target_pairs={{1,0},{2,1},{3,2},{4,3},{5,4},{6,5},{7,6},{8,7},{9,8},{10,9},{11,1... | collective-permute-start | bytes 393224 | tf_op jit(solution)/shard_map/ppermute | solution.py:26
  72.9 25.6 %copy-start.3 = (f32[64,1,127]{2,0,1:T(8,128)S(1)}, f32[64,1,127]{2,0,1:T(8,128)}, u32[]{:S(2)}) copy-start(f32[64,1,127]{2,0,1:T(8,128)} %get-tuple-element.44) | copy-start | bytes 97540
  73.0 51.2 %collective-permute-start.10 = (f32[1024,1,256]{0,2,1:T(8,128)S(1)}, f32[1024,1,256]{0,2,1:T(8,128)S(1)}, u32[]{:S(2)}, u32[]{:S(2)}) collective-permute-start(f32[1024,1,256]{0,2,1:T(8,128)S(1)} %bitcast.199), channel_id=1, source_target_pairs={{0,1},{1,2},{2,3},{3,4},{4,5},{5,6},{6,7},{7,8},{8,9},{9,10},{10,1... | collective-permute-start | bytes 3145736 | tf_op jit(solution)/shard_map/ppermute | solution.py:24
  97.5 26.7 %collective-permute-start.11 = (f32[1024,1,256]{0,2,1:T(8,128)S(1)}, f32[1024,1,256]{0,2,1:T(8,128)S(1)}, u32[]{:S(2)}, u32[]{:S(2)}) collective-permute-start(f32[1024,1,256]{0,2,1:T(8,128)S(1)} %bitcast.201), channel_id=1, source_target_pairs={{1,0},{2,1},{3,2},{4,3},{5,4},{6,5},{7,6},{8,7},{9,8},{10,9},{11,1... | collective-permute-start | bytes 3145736 | tf_op jit(solution)/shard_map/ppermute | solution.py:26
  99.6 21.0 %collective-permute-start.8 = (f32[2,128]{1,0:T(2,128)S(1)}, f32[2,128]{1,0:T(2,128)S(1)}, u32[]{:S(2)}, u32[]{:S(2)}) collective-permute-start(f32[2,128]{1,0:T(2,128)S(1)} %fusion.73), channel_id=1, source_target_pairs={{0,1},{1,2},{2,3},{3,4},{4,5},{5,6},{6,7},{7,8},{8,9},{9,10},{10,1... | collective-permute-start | bytes 3080 | tf_op jit(solution)/shard_map/ppermute | solution.py:24
  102.2 21.5 %collective-permute-start.9 = (f32[2,128]{1,0:T(2,128)S(1)}, f32[2,128]{1,0:T(2,128)S(1)}, u32[]{:S(2)}, u32[]{:S(2)}) collective-permute-start(f32[2,128]{1,0:T(2,128)S(1)} %fusion.73), channel_id=1, source_target_pairs={{1,0},{2,1},{3,2},{4,3},{5,4},{6,5},{7,6},{8,7},{9,8},{10,9},{11,1... | collective-permute-start | bytes 3080 | tf_op jit(solution)/shard_map/ppermute | solution.py:26
  105.1 39.0 %collective-permute-start.14 = (f32[64,1,128]{2,0,1:T(8,128)S(1)}, f32[64,1,128]{2,0,1:T(8,128)S(1)}, u32[]{:S(2)}, u32[]{:S(2)}) collective-permute-start(f32[64,1,128]{2,0,1:T(8,128)S(1)} %get-tuple-element.10), channel_id=1, source_target_pairs={{1,0},{2,1},{3,2},{4,3},{5,4},{6,5},{7,6},{8,7},{9,8},{10,9},{11,1... | collective-permute-start | bytes 98312 | tf_op jit(solution)/shard_map/ppermute | solution.py:26
  120.6 23.5 %collective-permute-start.15 = (f32[64,1,128]{2,0,1:T(8,128)S(1)}, f32[64,1,128]{2,0,1:T(8,128)S(1)}, u32[]{:S(2)}, u32[]{:S(2)}) collective-permute-start(f32[64,1,128]{2,0,1:T(8,128)S(1)} %get-tuple-element.10), channel_id=1, source_target_pairs={{0,1},{1,2},{2,3},{3,4},{4,5},{5,6},{6,7},{7,8},{8,9},{9,10},{10,1... | collective-permute-start | bytes 98312 | tf_op jit(solution)/shard_map/ppermute | solution.py:24
  134.2 8.9 %collective-permute-start.12 = (f32[128,256]{0,1:T(8,128)S(1)}, f32[128,256]{0,1:T(8,128)S(1)}, u32[]{:S(2)}, u32[]{:S(2)}) collective-permute-start(f32[128,256]{0,1:T(8,128)S(1)} %convolution_bitcast_fusion), channel_id=1, source_target_pairs={{0,1},{1,2},{2,3},{3,4},{4,5},{5,6},{6,7},{7,8},{8,9},{9,10},{10,1... | collective-permute-start | bytes 393224 | tf_op jit(solution)/shard_map/ppermute | solution.py:24
  137.1 6.1 %collective-permute-start.13 = (f32[128,256]{0,1:T(8,128)S(1)}, f32[128,256]{0,1:T(8,128)S(1)}, u32[]{:S(2)}, u32[]{:S(2)}) collective-permute-start(f32[128,256]{0,1:T(8,128)S(1)} %convolution_bitcast_fusion), channel_id=1, source_target_pairs={{1,0},{2,1},{3,2},{4,3},{5,4},{6,5},{7,6},{8,7},{9,8},{10,9},{11,1... | collective-permute-start | bytes 393224 | tf_op jit(solution)/shard_map/ppermute | solution.py:26
  (32 other events, 338.4 us)
where the time goes:
time: 146 us; the launch traced here: 145 us
  waiting for transfers between devices  68.2 us (47%)
  starting transfers between devices  32.8 us (22%)
  matrix products  21.5 us (15%)
  local copies, waits for them, and re-layouts  15 us (10%)
  other arithmetic  6.05 us (4%)
    ppermute x8, waiting for transfers between devices, padded_2(): lax.ppermute(tail, axis, [(i, (i + 1) % count) for i in range(count)])  67.6 us
    dot_general x8, matrix products, sources(): jnp.dot(quad_tables[config], rounded, preferred_element_type=jnp.float32)  17.6 us
    ppermute x8, starting transfers between devices, padded_2(): lax.ppermute(head, axis, [((i + 1) % count, i) for i in range(count)])  17 us
    ppermute x8, starting transfers between devices, padded_2(): lax.ppermute(tail, axis, [(i, (i + 1) % count) for i in range(count)])  15.8 us
    unnamed x83, local copies, waits for them, and re-layouts  3.97 us
  transfers between devices with their start and end apart: 16, of which 6 were waited for; matrix products, arithmetic and copies ran while one was open for 27% of the time, Pallas kernels for 0%

commit v1 on v0

v1 whole, which is shorter than its diff:
```python
import jax
import jax.numpy as jnp
from jax import lax
from jax.experimental import pallas as pl
from jax.experimental.pallas import tpu as pltpu
from jax.sharding import PartitionSpec as P

STEPS = 2
OCEAN_STEP = 0.5
COMM = 8
BLOCKS = 4
MESH = pl.DeviceIdType.MESH
HIGH = lax.Precision.HIGHEST


def wave_kernel(
    spec, wet, courant, sign, qidx, qwt, nonlinear, table, pidx, pwt, oidx, owt,
    currents, coriolis, mixing, sweight,
    spec_out, cur_out,
    araw, cols, quad, near, far, adv, advb, mid, midb, state,
    sflow, shalo, zhalo, obuf, ohalo, ptab, otab, dbuf, dhalo, dself, tan,
    sem1s, sem1r, sem2s, sem2r, ssend, srecv, zsend, zrecv, osend, orecv, dsend, drecv,
):
    comps, points = spec.shape
    cells = coriolis.shape[1]
    levels = mixing.shape[1]
    dev_count = lax.axis_size("dev")
    total = lax.axis_size("mp") * dev_count
    pos = lax.axis_index("mp") * dev_count + lax.axis_index("dev")
    odd = lax.rem(pos, 2)
    up = lax.rem(pos + 1, total)
    down = lax.rem(pos + total - 1, total)
    up2 = lax.rem(pos + 2, total)
    down2 = lax.rem(pos + total - 2, total)
    partner = pos + 1 - 2 * odd
    far_to = lax.rem(pos + 2 - 4 * odd + total, total)

    def where_is(p):
        return (lax.div(p, dev_count), lax.rem(p, dev_count))

    def remote(src, dst, ssem, rsem, p):
        return pltpu.make_async_remote_copy(
            src_ref=src, dst_ref=dst, send_sem=ssem, recv_sem=rsem,
            device_id=where_is(p), device_id_type=MESH,
        )

    size = comps // COMM

    def rows(c):
        return pl.ds(pl.multiple_of(c * size, size), size)

    def swap(step, c):
        src = spec if step == 0 else mid
        return remote(src.at[rows(c)], near.at[step, rows(c)], sem1s.at[step, c], sem1r.at[step, c], partner)

    def relay(step, c):
        return remote(near.at[step, rows(c)], far.at[step, rows(c)], sem2s.at[step, c], sem2r.at[step, c], far_to)

    def pair(src_up, src_down, halo, ssem, rsem, step):
        return (
            remote(src_up, halo.at[step, 0], ssem.at[step, 0], rsem.at[step, 0], up),
            remote(src_down, halo.at[step, 1], ssem.at[step, 1], rsem.at[step, 1], down),
        )

    def surface_pair(step):
        return pair(sflow.at[step], sflow.at[step], shalo, ssend, srecv, step)

    def zonal_pair(step):
        src = currents.at[0] if step == 0 else state.at[0]
        return pair(src, src, zhalo, zsend, zrecv, step)

    def index_pair():
        return pair(obuf, obuf, ohalo, osend, orecv, 0)

    def drift_pair(step):
        return pair(dbuf.at[step, 0], dbuf.at[step, 1], dhalo, dsend, drecv, step)

    def start(copies):
        for copy in copies:
            copy.start()

    def received(copies):
        for copy in copies:
            copy.wait_recv()

    def sent(copies):
        for copy in copies:
            copy.wait_send()

    def each(low, high, body):
        def run(c, carry):
            body(c)
            return carry

        lax.fori_loop(low, high, run, 0)

    barrier = pltpu.get_barrier_semaphore()
    for p in (up, down, up2, down2):
        pl.semaphore_signal(barrier, inc=1, device_id=where_is(p), device_id_type=MESH)
    pl.semaphore_wait(barrier, 4)

    each(0, COMM, lambda c: swap(0, c).start())
    start(zonal_pair(0))
    obuf[0:4, :] = oidx[...].astype(jnp.float32)
    obuf[4:8, :] = owt[...]

    araw[...] = jnp.zeros_like(araw)
    araw[0:2, :] = courant[...]
    araw[2:4, :] = (2 * sign[...] - 1).astype(jnp.float32)
    araw[4:5, :] = nonlinear[...]
    araw[5:6, 0:levels] = mixing[...]
    araw[6:7, 0:levels] = sweight[...]
    araw[8:16, :] = qidx[...].astype(jnp.float32)
    araw[16:24, :] = qwt[...]
    cols[...] = jnp.transpose(araw[...])
    sflow[...] = jnp.zeros_like(sflow)
    level_mix = cols[0:levels, 5:6]
    level_weight = cols[0:levels, 6:7]

    def surface(source, step):
        for a in range(2):
            sflow[step, a : a + 1, :] = jnp.sum(level_weight * source[a], axis=0, keepdims=True)

    surface(currents, 0)
    start(index_pair())
    start(surface_pair(0))

    lanes = lax.broadcasted_iota(jnp.int32, (32, comps), 1).astype(jnp.float32)

    def build_quad(c):
        for sub in range(size // 32):
            at = pl.ds(pl.multiple_of(c * size + sub * 32, 32), 32)
            col = cols[at, :]
            for j in range(4):
                one = jnp.where(col[:, 8 + 2 * j : 9 + 2 * j] == lanes, col[:, 16 + 2 * j : 17 + 2 * j], 0.0)
                two = jnp.where(col[:, 9 + 2 * j : 10 + 2 * j] == lanes, col[:, 17 + 2 * j : 18 + 2 * j], 0.0)
                quad[j, at, :] = (one + two).astype(jnp.bfloat16)

    def forward(step):
        def body(c):
            swap(step, c).wait_recv()
            relay(step, c).start()

        return body

    def first(c):
        build_quad(c)
        forward(0)(c)

    each(0, COMM, first)

    slots = lax.broadcasted_iota(jnp.int32, (cells, points), 0)
    for q, owner in enumerate((down, pos, up)):
        acc = jnp.zeros((cells, points), jnp.float32)
        for j in range(4):
            acc = acc + jnp.where(pidx[j : j + 1, :] - owner * cells == slots, pwt[j : j + 1, :], 0.0)
        ptab[q] = acc
    received(index_pair())
    oslots = lax.broadcasted_iota(jnp.int32, (points, cells), 0).astype(jnp.float32)
    base = (pos * points).astype(jnp.float32)
    for q in range(3):
        source = obuf[...] if q == 2 else ohalo[0, q]
        acc = jnp.zeros((points, cells), jnp.float32)
        for j in range(4):
            acc = acc + jnp.where(source[j : j + 1, :] - base == oslots, source[4 + j : 5 + j, :], 0.0)
        otab[q] = acc

    parity = (1 - 2 * odd).astype(jnp.float32)

    def flow(step):
        received(surface_pair(step))
        total_flow = jnp.dot(shalo[step, 0], ptab[0], precision=HIGH, preferred_element_type=jnp.float32)
        total_flow += jnp.dot(sflow[step], ptab[1], precision=HIGH, preferred_element_type=jnp.float32)
        total_flow += jnp.dot(shalo[step, 1], ptab[2], precision=HIGH, preferred_element_type=jnp.float32)
        tan[...] = jnp.tanh(total_flow)

    def advect(step):
        source = spec if step == 0 else mid

        def body(c):
            relay(step, c).wait_recv()
            at = rows(c)
            own = source[at, :]
            col = cols[at, :]
            sense_x = col[:, 2:3]
            sense_y = col[:, 3:4]
            behind_x = jnp.where(sense_x > 0, pltpu.roll(own, 1, 1), pltpu.roll(own, points - 1, 1))
            behind_y = jnp.where(sense_y * parity > 0, far[step, at, :], near[step, at, :])
            speed_x = col[:, 0:1] * (1.0 + 0.5 * (sense_x * tan[0:1, :]))
            speed_y = col[:, 1:2] * (1.0 + 0.5 * (sense_y * tan[1:2, :]))
            value = own - speed_x * (own - behind_x) - speed_y * (own - behind_y)
            adv[at, :] = value
            advb[at, :] = value.astype(jnp.bfloat16)

        each(0, COMM, body)

    wide = comps // BLOCKS
    wet_row = wet[...].astype(jnp.float32)

    def source_block(step):
        target = mid if step == 0 else spec_out

        def body(r):
            at = pl.ds(pl.multiple_of(r * wide, wide), wide)
            terms = [
                jnp.dot(quad[j, at, :], advb[...], preferred_element_type=jnp.float32) for j in range(4)
            ]
            value = adv[at, :]
            total_sum = terms[0] + terms[1] + terms[2] + terms[3]
            pair_sum = terms[0] * terms[1] + terms[2] * terms[3]
            new = wet_row * (value + cols[at, 4:5] * (value * value * total_sum - value * pair_sum))
            target[at, :] = new
            midb[at, :] = new.astype(jnp.bfloat16)

        return body

    def drift_parts(step):
        stokes = jnp.dot(table[...], midb[...], preferred_element_type=jnp.float32)
        dbuf[step, 0] = jnp.dot(stokes, otab[1], precision=HIGH, preferred_element_type=jnp.float32)
        dbuf[step, 1] = jnp.dot(stokes, otab[0], precision=HIGH, preferred_element_type=jnp.float32)
        start(drift_pair(step))
        dself[...] = jnp.dot(stokes, otab[2], precision=HIGH, preferred_element_type=jnp.float32)

    level_row = lax.broadcasted_iota(jnp.int32, (levels, cells), 0)

    def mix(w):
        above = jnp.where(level_row == 0, w, pltpu.roll(w, 1, 0))
        below = jnp.where(level_row == levels - 1, w, pltpu.roll(w, levels - 1, 0))
        return level_mix * (above - 2.0 * w + below)

    def ocean(step):
        received(drift_pair(step))
        received(zonal_pair(step))
        source = currents if step == 0 else state
        target = state if step == 0 else cur_out
        drift = dself[...] + dhalo[step, 0] + dhalo[step, 1]
        drift_x, drift_y = drift[0:levels], drift[levels : 2 * levels]
        u, v = source[0], source[1]
        rot = coriolis[...]
        turn = 0.5 * (pltpu.roll(v, cells - 1, 1) - pltpu.roll(v, 1, 1)) - 0.5 * (zhalo[step, 1] - zhalo[step, 0])
        new_u = u + OCEAN_STEP * (rot * (v + drift_y) + turn * drift_y + mix(u))
        new_v = v + OCEAN_STEP * (-rot * (u + drift_x) - turn * drift_x + mix(v))
        target[0] = new_u
        target[1] = new_v

    flow(0)
    advect(0)
    source_block(0)(0)
    per = COMM // BLOCKS
    each(0, per, lambda c: swap(1, c).start())
    each(1, BLOCKS, source_block(0))
    drift_parts(0)
    each(per, COMM, lambda c: swap(1, c).start())
    each(0, COMM - 3, forward(1))
    ocean(0)
    surface(state, 1)
    start(surface_pair(1))
    start(zonal_pair(1))
    each(COMM - 3, COMM, forward(1))
    flow(1)
    advect(1)
    each(0, BLOCKS, source_block(1))
    drift_parts(1)
    ocean(1)

    sent(index_pair())
    for step in range(STEPS):
        each(0, COMM, lambda c: swap(step, c).wait_send())
        each(0, COMM, lambda c: relay(step, c).wait_send())
        sent(surface_pair(step))
        sent(zonal_pair(step))
        sent(drift_pair(step))


def local(
    spectrum, water_mask, courant, stencil_sign, quad_index, quad_weight, nonlinear, stokes_table,
    point_index, point_weight, ocean_index, ocean_weight, currents, coriolis, mixing, surface_weights,
):
    comps, points = spectrum.shape
    levels, cells = currents.shape[1:]
    f32, bf16 = jnp.float32, jnp.bfloat16
    vm = pl.BlockSpec(memory_space=pltpu.VMEM)
    dma = pltpu.SemaphoreType.DMA
    scratch = [
        pltpu.VMEM((128, comps), f32),
        pltpu.VMEM((comps, 128), f32),
        pltpu.VMEM((4, comps, comps), bf16),
        pltpu.VMEM((STEPS, comps, points), f32),
        pltpu.VMEM((STEPS, comps, points), f32),
        pltpu.VMEM((comps, points), f32),
        pltpu.VMEM((comps, points), bf16),
        pltpu.VMEM((comps, points), f32),
        pltpu.VMEM((comps, points), bf16),
        pltpu.VMEM((2, levels, cells), f32),
        pltpu.VMEM((STEPS, 8, cells), f32),
        pltpu.VMEM((STEPS, 2, 8, cells), f32),
        pltpu.VMEM((STEPS, 2, levels, cells), f32),
        pltpu.VMEM((8, cells), f32),
        pltpu.VMEM((1, 2, 8, cells), f32),
        pltpu.VMEM((3, cells, points), f32),
        pltpu.VMEM((3, points, cells), f32),
        pltpu.VMEM((STEPS, 2, 2 * levels, cells), f32),
        pltpu.VMEM((STEPS, 2, 2 * levels, cells), f32),
        pltpu.VMEM((2 * levels, cells), f32),
        pltpu.VMEM((8, points), f32),
        dma((STEPS, COMM)),
        dma((STEPS, COMM)),
        dma((STEPS, COMM)),
        dma((STEPS, COMM)),
    ] + [dma((n, 2)) for n in (STEPS, STEPS, STEPS, STEPS, 1, 1, STEPS, STEPS)]
    return pl.pallas_call(
        wave_kernel,
        out_shape=(
            jax.ShapeDtypeStruct((comps, points), f32),
            jax.ShapeDtypeStruct(currents.shape, f32),
        ),
        in_specs=[vm] * 16,
        out_specs=(vm, vm),
        scratch_shapes=scratch,
        compiler_params=pltpu.CompilerParams(
            collective_id=0, has_side_effects=True, vmem_limit_bytes=56 * 1024 * 1024
        ),
    )(
        spectrum,
        water_mask.reshape(1, points),
        courant,
        stencil_sign,
        quad_index.transpose(0, 2, 1).reshape(8, comps),
        quad_weight.transpose(0, 2, 1).reshape(8, comps),
        nonlinear.reshape(1, comps),
        stokes_table,
        point_index,
        point_weight,
        ocean_index,
        ocean_weight,
        currents,
        coriolis.reshape(1, cells),
        mixing.reshape(1, levels),
        surface_weights.reshape(1, levels),
    )


def solution(mesh):
    ring = P(("mp", "dev"))
    split = P(None, ("mp", "dev"))
    deep = P(None, None, ("mp", "dev"))
    return jax.shard_map(
        local,
        mesh=mesh,
        in_specs=(
            split, ring, P(), P(), P(), P(), P(), P(), split, split, split, split, deep, ring, P(), P(),
        ),
        out_specs=(split, deep),
        check_vma=False,
    )
```

time: 146 us -> 88.8 us (0.61)
  Pallas kernels: 0 us -> 82.9 us
  waiting for transfers between devices: 68.2 us -> 0 us
  starting transfers between devices: 32.8 us -> 0 us
  matrix products: 21.5 us -> 0 us
  local copies, waits for them, and re-layouts: 15 us -> 4.97 us
  other arithmetic: 6.05 us -> 0 us
    pallas_call x0 -> x1, Pallas kernels: none -> 82.9 us  [local(): pl.pallas_call(wave_kernel, out_shape=(jax.ShapeDtypeStruct((comps, point...]
    ppermute x16 -> x0, waiting for transfers between devices: 68.2 us -> none  [the longest x8 67.6 us: padded_2(): lax.ppermute(tail, axis, [(i, (i + 1) % count) for i in range(count)])]
    ppermute x16 -> x0, starting transfers between devices: 32.8 us -> none  [the longest x8 17 us: padded_2(): lax.ppermute(head, axis, [((i + 1) % count, i) for i in range(count)])]
    dot_general x14 -> x0, matrix products: 21.5 us -> none  [the longest x8 17.6 us: sources(): jnp.dot(quad_tables[config], rounded, preferred_element_type=jnp.float32)]
    slice x17 -> x0, local copies, waits for them, and re-layouts: 5.18 us -> none  [the longest x4 2.39 us: quad_table(): first_part = jnp.where(row_index[:, 0:1] == columns, weight[:, 0:1], 0.0)]
    squeeze x2 -> x0, local copies, waits for them, and re-layouts: 2.71 us -> none  [the longest x1 1.36 us: local(): quad_index[config]]
    reshape x0 -> x2, local copies, waits for them, and re-layouts: none -> 2.04 us  [the longest x1 1.4 us: local(): quad_index.transpose(0, 2, 1).reshape(8, comps)]
    convert_element_type x4 -> x0, other arithmetic: 1.88 us -> none  [the longest x2 1.87 us: sources(): rounded = advected.astype(jnp.bfloat16)]
  transfers between devices with their start and end apart: 16 -> 0, of which waited for: 6 -> 0; matrix products, arithmetic and copies ran while one was open for 27% -> 0% of each run, Pallas kernels for 0% -> 0%
where the time goes in v1:
time: 88.8 us; the launch traced here: 88.5 us
  Pallas kernels  82.9 us (93%)
  local copies, waits for them, and re-layouts  4.97 us (6%)
    pallas_call x1, Pallas kernels, local(): pl.pallas_call(wave_kernel, out_shape=(jax.ShapeDtypeStruct((comps, point...  82.9 us
    unnamed x6, local copies, waits for them, and re-layouts  2.93 us

profile of v1, /device:TPU:0, one launch (start us, length us, event | category | flops | bytes accessed | tf_op | source)
XLA Modules:
  0.0 88.5 jit_solution(3162493680444715642)
XLA Ops:
  0.6 0.0 copy-start.1
  0.6 1.4 %reshape.26.qidx = s32[8,1024]{1,0:T(8,128)} reshape(s32[4,2,1024]{2,1,0:T(2,128)} %bitcast.7) | data formatting | bytes 65536 | tf_op jit(solution)/shard_map/reshape | solution.py:328
  2.0 0.0 copy-done.1
  2.0 0.6 reshape.27.qwt
  2.7 82.9 %shard_map.167 = (f32[1024,256]{1,0:T(8,128)}, f32[2,64,128]{2,1,0:T(8,128)}) custom-call(f32[1024,256]{1,0:T(8,128)} %spec.1, s32[1,256]{1,0:T(1,128)} %bitcast.10, f32[2,1024]{1,0:T(2,128)} %courant.1, s32[2,1024]{1,0:T(2,128)} %sign.1, s32[8,1024]{1,0:T(8,128)} %reshape.26.qidx, f32[8,1024]{1,0:T(8,128)} %reshape.27.qwt, f32[1,1024]{1,0:T(1,128)} %bitcast.9, ...), custom_call_target="tpu_custom_call" | custom-call | tf_op jit(solution)/shard_map/pallas_call | solution.py:311
  85.6 0.0 copy-start
  85.6 2.3 %copy.20 = f32[1024,256]{1,0:T(8,128)} copy(f32[1024,256]{1,0:T(8,128)} %get-tuple-element.4) | data formatting | bytes 2097152
  87.9 0.0 copy-done
  87.9 0.6 copy.21
Async XLA Ops:
  0.6 1.4 %copy-start.1 = (f32[4,1024,2]{1,2,0:T(2,128)S(1)}, f32[4,1024,2]{1,2,0:T(2,128)}, u32[]{:S(2)}) copy-start(f32[4,1024,2]{1,2,0:T(2,128)} %param.21) | copy-start | bytes 98308
  85.6 2.3 %copy-start = (f32[2,64,128]{2,1,0:T(8,128)S(1)}, f32[2,64,128]{2,1,0:T(8,128)}, u32[]{:S(2)}) copy-start(f32[2,64,128]{2,1,0:T(8,128)} %get-tuple-element.5) | copy-start | bytes 196612

commit v2 on v1

--- a/solution.py
+++ b/solution.py
@@ -7,7 +7,7 @@
 
 STEPS = 2
 OCEAN_STEP = 0.5
-COMM = 8
+COMM = 16
 BLOCKS = 4
 MESH = pl.DeviceIdType.MESH
 HIGH = lax.Precision.HIGHEST
@@ -18,7 +18,7 @@
     currents, coriolis, mixing, sweight,
     spec_out, cur_out,
     araw, cols, quad, near, far, adv, advb, mid, midb, state,
-    sflow, shalo, zhalo, obuf, ohalo, ptab, otab, dbuf, dhalo, dself, tan,
+    sflow, shalo, zhalo, obuf, ohalo, ptab, otab, dbuf, dhalo, dself, tan, acc,
     sem1s, sem1r, sem2s, sem2r, ssend, srecv, zsend, zrecv, osend, orecv, dsend, drecv,
 ):
     comps, points = spec.shape
@@ -110,8 +110,9 @@
     araw[4:5, :] = nonlinear[...]
     araw[5:6, 0:levels] = mixing[...]
     araw[6:7, 0:levels] = sweight[...]
-    araw[8:16, :] = qidx[...].astype(jnp.float32)
-    araw[16:24, :] = qwt[...]
+    for j in range(4):
+        araw[8 + 2 * j : 10 + 2 * j, :] = qidx[j].astype(jnp.float32)
+        araw[16 + 2 * j : 18 + 2 * j, :] = qwt[j]
     cols[...] = jnp.transpose(araw[...])
     sflow[...] = jnp.zeros_like(sflow)
     level_mix = cols[0:levels, 5:6]
@@ -128,8 +129,8 @@
     lanes = lax.broadcasted_iota(jnp.int32, (32, comps), 1).astype(jnp.float32)
 
     def build_quad(c):
-        for sub in range(size // 32):
-            at = pl.ds(pl.multiple_of(c * size + sub * 32, 32), 32)
+        for sub in range(2 * size // 32):
+            at = pl.ds(pl.multiple_of(c * 2 * size + sub * 32, 32), 32)
             col = cols[at, :]
             for j in range(4):
                 one = jnp.where(col[:, 8 + 2 * j : 9 + 2 * j] == lanes, col[:, 16 + 2 * j : 17 + 2 * j], 0.0)
@@ -147,23 +148,23 @@
         build_quad(c)
         forward(0)(c)
 
-    each(0, COMM, first)
+    each(0, COMM // 2, first)
 
     slots = lax.broadcasted_iota(jnp.int32, (cells, points), 0)
     for q, owner in enumerate((down, pos, up)):
-        acc = jnp.zeros((cells, points), jnp.float32)
+        spread = jnp.zeros((cells, points), jnp.float32)
         for j in range(4):
-            acc = acc + jnp.where(pidx[j : j + 1, :] - owner * cells == slots, pwt[j : j + 1, :], 0.0)
-        ptab[q] = acc
+            spread = spread + jnp.where(pidx[j : j + 1, :] - owner * cells == slots, pwt[j : j + 1, :], 0.0)
+        ptab[q] = spread
     received(index_pair())
     oslots = lax.broadcasted_iota(jnp.int32, (points, cells), 0).astype(jnp.float32)
     base = (pos * points).astype(jnp.float32)
     for q in range(3):
         source = obuf[...] if q == 2 else ohalo[0, q]
-        acc = jnp.zeros((points, cells), jnp.float32)
+        spread = jnp.zeros((points, cells), jnp.float32)
         for j in range(4):
-            acc = acc + jnp.where(source[j : j + 1, :] - base == oslots, source[4 + j : 5 + j, :], 0.0)
-        otab[q] = acc
+            spread = spread + jnp.where(source[j : j + 1, :] - base == oslots, source[4 + j : 5 + j, :], 0.0)
+        otab[q] = spread
 
     parity = (1 - 2 * odd).astype(jnp.float32)
 
@@ -173,6 +174,13 @@
         total_flow += jnp.dot(sflow[step], ptab[1], precision=HIGH, preferred_element_type=jnp.float32)
         total_flow += jnp.dot(shalo[step, 1], ptab[2], precision=HIGH, preferred_element_type=jnp.float32)
         tan[...] = jnp.tanh(total_flow)
+
+    wide = comps // BLOCKS
+    per = COMM // BLOCKS
+    wet_row = wet[...].astype(jnp.float32)
+
+    def block(r):
+        return pl.ds(pl.multiple_of(r * wide, wide), wide)
 
     def advect(step):
         source = spec if step == 0 else mid
@@ -192,19 +200,31 @@
             adv[at, :] = value
             advb[at, :] = value.astype(jnp.bfloat16)
 
-        each(0, COMM, body)
-
-    wide = comps // BLOCKS
-    wet_row = wet[...].astype(jnp.float32)
-
-    def source_block(step):
+        return body
+
+    def gather(step, g):
+        each(g * per, (g + 1) * per, advect(step))
+        part = advb[g * wide : (g + 1) * wide, :]
+
+        def body(r):
+            at = block(r)
+            for j in range(4):
+                term = jnp.dot(
+                    quad[j, at, g * wide : (g + 1) * wide], part, preferred_element_type=jnp.float32
+                )
+                if g == 0:
+                    acc[j, at, :] = term
+                else:
+                    acc[j, at, :] += term
+
+        each(0, BLOCKS, body)
+
+    def finish(step):
         target = mid if step == 0 else spec_out
 
         def body(r):
-            at = pl.ds(pl.multiple_of(r * wide, wide), wide)
-            terms = [
-                jnp.dot(quad[j, at, :], advb[...], preferred_element_type=jnp.float32) for j in range(4)
-            ]
+            at = rows(r)
+            terms = [acc[j, at, :] for j in range(4)]
             value = adv[at, :]
             total_sum = terms[0] + terms[1] + terms[2] + terms[3]
             pair_sum = terms[0] * terms[1] + terms[2] * terms[3]
@@ -216,9 +236,11 @@
 
     def drift_parts(step):
         stokes = jnp.dot(table[...], midb[...], preferred_element_type=jnp.float32)
+        ahead, behind = drift_pair(step)
         dbuf[step, 0] = jnp.dot(stokes, otab[1], precision=HIGH, preferred_element_type=jnp.float32)
+        ahead.start()
         dbuf[step, 1] = jnp.dot(stokes, otab[0], precision=HIGH, preferred_element_type=jnp.float32)
-        start(drift_pair(step))
+        behind.start()
         dself[...] = jnp.dot(stokes, otab[2], precision=HIGH, preferred_element_type=jnp.float32)
 
     level_row = lax.broadcasted_iota(jnp.int32, (levels, cells), 0)
@@ -229,37 +251,48 @@
         return level_mix * (above - 2.0 * w + below)
 
     def ocean(step):
-        received(drift_pair(step))
-        received(zonal_pair(step))
         source = currents if step == 0 else state
         target = state if step == 0 else cur_out
-        drift = dself[...] + dhalo[step, 0] + dhalo[step, 1]
-        drift_x, drift_y = drift[0:levels], drift[levels : 2 * levels]
+        received(zonal_pair(step))
         u, v = source[0], source[1]
         rot = coriolis[...]
         turn = 0.5 * (pltpu.roll(v, cells - 1, 1) - pltpu.roll(v, 1, 1)) - 0.5 * (zhalo[step, 1] - zhalo[step, 0])
-        new_u = u + OCEAN_STEP * (rot * (v + drift_y) + turn * drift_y + mix(u))
-        new_v = v + OCEAN_STEP * (-rot * (u + drift_x) - turn * drift_x + mix(v))
+        mix_u, mix_v = mix(u), mix(v)
+        received(drift_pair(step))
+        drift = dself[...] + dhalo[step, 0] + dhalo[step, 1]
+        drift_x, drift_y = drift[0:levels], drift[levels : 2 * levels]
+        new_u = u + OCEAN_STEP * (rot * (v + drift_y) + turn * drift_y + mix_u)
+        new_v = v + OCEAN_STEP * (-rot * (u + drift_x) - turn * drift_x + mix_v)
         target[0] = new_u
         target[1] = new_v
 
+    half = COMM // 2
     flow(0)
-    advect(0)
-    source_block(0)(0)
-    per = COMM // BLOCKS
+    gather(0, 0)
+    each(half, half + per, forward(0))
+    gather(0, 1)
+    each(half + per, COMM, forward(0))
+    gather(0, 2)
+    gather(0, 3)
+    each(0, per, finish(0))
     each(0, per, lambda c: swap(1, c).start())
-    each(1, BLOCKS, source_block(0))
+    each(per, COMM, finish(0))
     drift_parts(0)
     each(per, COMM, lambda c: swap(1, c).start())
-    each(0, COMM - 3, forward(1))
+    each(0, per + 1, forward(1))
     ocean(0)
     surface(state, 1)
     start(surface_pair(1))
     start(zonal_pair(1))
-    each(COMM - 3, COMM, forward(1))
+    each(per + 1, half, forward(1))
     flow(1)
-    advect(1)
-    each(0, BLOCKS, source_block(1))
+    gather(1, 0)
+    each(half, half + per, forward(1))
+    gather(1, 1)
+    each(half + per, COMM, forward(1))
+    gather(1, 2)
+    gather(1, 3)
+    each(0, COMM, finish(1))
     drift_parts(1)
     ocean(1)
 
@@ -303,6 +336,7 @@
         pltpu.VMEM((STEPS, 2, 2 * levels, cells), f32),
         pltpu.VMEM((2 * levels, cells), f32),
         pltpu.VMEM((8, points), f32),
+        pltpu.VMEM((4, comps, points), f32),
         dma((STEPS, COMM)),
         dma((STEPS, COMM)),
         dma((STEPS, COMM)),
@@ -311,8 +345,8 @@
     return pl.pallas_call(
         wave_kernel,
         out_shape=(
-            jax.ShapeDtypeStruct((comps, points), f32),
-            jax.ShapeDtypeStruct(currents.shape, f32),
+            pltpu.VMEM((comps, points), f32),
+            pltpu.VMEM(currents.shape, f32),
         ),
         in_specs=[vm] * 16,
         out_specs=(vm, vm),
@@ -325,8 +359,8 @@
         water_mask.reshape(1, points),
         courant,
         stencil_sign,
-        quad_index.transpose(0, 2, 1).reshape(8, comps),
-        quad_weight.transpose(0, 2, 1).reshape(8, comps),
+        quad_index.transpose(0, 2, 1),
+        quad_weight.transpose(0, 2, 1),
         nonlinear.reshape(1, comps),
         stokes_table,
         point_index,

time: 88.8 us -> 106 us (1.19)
  Pallas kernels: 82.9 us -> 103 us
  local copies, waits for them, and re-layouts: 4.97 us -> 1.6 us
    pallas_call x1, Pallas kernels: 82.9 us -> 103 us  [local(): pl.pallas_call(wave_kernel, out_shape=(pltpu.VMEM((comps, points), f32),...]
    reshape x2 -> x0, local copies, waits for them, and re-layouts: 2.04 us -> none  [the longest x1 1.4 us: local(): quad_index.transpose(0, 2, 1).reshape(8, comps)]
    unnamed x6 -> x2, local copies, waits for them, and re-layouts: 2.93 us -> 1.6 us
where the time goes in v2:
time: 106 us
  Pallas kernels  103 us (97%)
  local copies, waits for them, and re-layouts  1.6 us (2%)
    pallas_call x1, Pallas kernels, local(): pl.pallas_call(wave_kernel, out_shape=(pltpu.VMEM((comps, points), f32),...  103 us

profile of v2, /device:TPU:0, one launch (start us, length us, event | category | flops | bytes accessed | tf_op | source)
XLA Modules:
  0.0 105.7 jit_solution(11702684577743048890)
XLA Ops:
  0.6 103.4 %shard_map.167 = (f32[1024,256]{1,0:T(8,128)S(1)}, f32[2,64,128]{2,1,0:T(8,128)S(1)}) custom-call(f32[1024,256]{1,0:T(8,128)} %spec.1, s32[1,256]{1,0:T(1,128)} %bitcast.10, f32[2,1024]{1,0:T(2,128)} %courant.1, s32[2,1024]{1,0:T(2,128)} %sign.1, s32[4,2,1024]{2,1,0:T(2,128)} %bitcast.7, f32[4,2,1024]{2,1,0:T(2,128)} %bitcast.8, f32[1,1024]{1,0:T(1,128)} %bitcast.9, ...), custom_call_target="tpu_custom_call" | custom-call | tf_op jit(solution)/shard_map/pallas_call | solution.py:345
  104.1 1.0 copy.20
  105.0 0.6 copy.21

commit v3 on v1

--- a/solution.py
+++ b/solution.py
@@ -110,8 +110,9 @@
     araw[4:5, :] = nonlinear[...]
     araw[5:6, 0:levels] = mixing[...]
     araw[6:7, 0:levels] = sweight[...]
-    araw[8:16, :] = qidx[...].astype(jnp.float32)
-    araw[16:24, :] = qwt[...]
+    for j in range(4):
+        araw[8 + 2 * j : 10 + 2 * j, :] = qidx[j].astype(jnp.float32)
+        araw[16 + 2 * j : 18 + 2 * j, :] = qwt[j]
     cols[...] = jnp.transpose(araw[...])
     sflow[...] = jnp.zeros_like(sflow)
     level_mix = cols[0:levels, 5:6]
@@ -216,9 +217,11 @@
 
     def drift_parts(step):
         stokes = jnp.dot(table[...], midb[...], preferred_element_type=jnp.float32)
+        ahead, behind = drift_pair(step)
         dbuf[step, 0] = jnp.dot(stokes, otab[1], precision=HIGH, preferred_element_type=jnp.float32)
+        ahead.start()
         dbuf[step, 1] = jnp.dot(stokes, otab[0], precision=HIGH, preferred_element_type=jnp.float32)
-        start(drift_pair(step))
+        behind.start()
         dself[...] = jnp.dot(stokes, otab[2], precision=HIGH, preferred_element_type=jnp.float32)
 
     level_row = lax.broadcasted_iota(jnp.int32, (levels, cells), 0)
@@ -229,17 +232,18 @@
         return level_mix * (above - 2.0 * w + below)
 
     def ocean(step):
-        received(drift_pair(step))
-        received(zonal_pair(step))
         source = currents if step == 0 else state
         target = state if step == 0 else cur_out
-        drift = dself[...] + dhalo[step, 0] + dhalo[step, 1]
-        drift_x, drift_y = drift[0:levels], drift[levels : 2 * levels]
+        received(zonal_pair(step))
         u, v = source[0], source[1]
         rot = coriolis[...]
         turn = 0.5 * (pltpu.roll(v, cells - 1, 1) - pltpu.roll(v, 1, 1)) - 0.5 * (zhalo[step, 1] - zhalo[step, 0])
-        new_u = u + OCEAN_STEP * (rot * (v + drift_y) + turn * drift_y + mix(u))
-        new_v = v + OCEAN_STEP * (-rot * (u + drift_x) - turn * drift_x + mix(v))
+        mix_u, mix_v = mix(u), mix(v)
+        received(drift_pair(step))
+        drift = dself[...] + dhalo[step, 0] + dhalo[step, 1]
+        drift_x, drift_y = drift[0:levels], drift[levels : 2 * levels]
+        new_u = u + OCEAN_STEP * (rot * (v + drift_y) + turn * drift_y + mix_u)
+        new_v = v + OCEAN_STEP * (-rot * (u + drift_x) - turn * drift_x + mix_v)
         target[0] = new_u
         target[1] = new_v
 
@@ -311,8 +315,8 @@
     return pl.pallas_call(
         wave_kernel,
         out_shape=(
-            jax.ShapeDtypeStruct((comps, points), f32),
-            jax.ShapeDtypeStruct(currents.shape, f32),
+            pltpu.VMEM((comps, points), f32),
+            pltpu.VMEM(currents.shape, f32),
         ),
         in_specs=[vm] * 16,
         out_specs=(vm, vm),
@@ -325,8 +329,8 @@
         water_mask.reshape(1, points),
         courant,
         stencil_sign,
-        quad_index.transpose(0, 2, 1).reshape(8, comps),
-        quad_weight.transpose(0, 2, 1).reshape(8, comps),
+        quad_index.transpose(0, 2, 1),
+        quad_weight.transpose(0, 2, 1),
         nonlinear.reshape(1, comps),
         stokes_table,
         point_index,

time: 88.8 us -> 84.2 us (0.948)
  local copies, waits for them, and re-layouts: 4.97 us -> 1.6 us
  Pallas kernels: 82.9 us -> 81.8 us
    reshape x2 -> x0, local copies, waits for them, and re-layouts: 2.04 us -> none  [the longest x1 1.4 us: local(): quad_index.transpose(0, 2, 1).reshape(8, comps)]
    unnamed x6 -> x2, local copies, waits for them, and re-layouts: 2.93 us -> 1.6 us
    pallas_call x1, Pallas kernels: 82.9 us -> 81.8 us  [local(): pl.pallas_call(wave_kernel, out_shape=(pltpu.VMEM((comps, points), f32),...]
where the time goes in v3:
time: 84.2 us; the launch traced here: 84 us
  Pallas kernels  81.8 us (97%)
  local copies, waits for them, and re-layouts  1.6 us (2%)
    pallas_call x1, Pallas kernels, local(): pl.pallas_call(wave_kernel, out_shape=(pltpu.VMEM((comps, points), f32),...  81.8 us

profile of v3, /device:TPU:0, one launch (start us, length us, event | category | flops | bytes accessed | tf_op | source)
XLA Modules:
  0.0 84.0 jit_solution(2591963251407553469)
XLA Ops:
  0.6 81.8 %shard_map.167 = (f32[1024,256]{1,0:T(8,128)S(1)}, f32[2,64,128]{2,1,0:T(8,128)S(1)}) custom-call(f32[1024,256]{1,0:T(8,128)} %spec.1, s32[1,256]{1,0:T(1,128)} %bitcast.10, f32[2,1024]{1,0:T(2,128)} %courant.1, s32[2,1024]{1,0:T(2,128)} %sign.1, s32[4,2,1024]{2,1,0:T(2,128)} %bitcast.7, f32[4,2,1024]{2,1,0:T(2,128)} %bitcast.8, f32[1,1024]{1,0:T(1,128)} %bitcast.9, ...), custom_call_target="tpu_custom_call" | custom-call | tf_op jit(solution)/shard_map/pallas_call | solution.py:315
  82.4 1.0 %copy.20 = f32[1024,256]{1,0:T(8,128)} copy(f32[1024,256]{1,0:T(8,128)S(1)} %get-tuple-element.2) | data formatting | bytes 2097152
  83.4 0.6 copy.21
